TPU v7x, 32 devices: a whole 2x2x4 slice. The times are simulated.
32 devices in a mesh: section: 2 (over x), outer: 4 (over y, core), tensor: 4 (over z).
Axes of the slice: x: 2, y: 2, z: 4, core: 2. Of those that a mesh axis runs over, the one named last changes fastest.
Arguments:
- act_in: bfloat16 [2, 16, 8192], P('section', 'outer', 'tensor'), may hold values from -6 to 6
- saved_in: bfloat16 [2, 16, 8192], P('section', 'outer', 'tensor'), may hold values from -6 to 6
- cotangent: bfloat16 [2, 16, 8192], P('section', 'outer', 'tensor'), may hold values from -6 to 6
- w_gate: bfloat16 [2, 8192, 14336], P('section', 'tensor', 'outer'), may hold values from -0.0625 to 0.0625
- w_up: bfloat16 [2, 8192, 14336], P('section', 'tensor', 'outer'), may hold values from -0.0625 to 0.0625
- w_down: bfloat16 [2, 14336, 8192], P('section', 'outer', 'tensor'), may hold values from -0.046875 to 0.046875
Outputs:
- forward_sent: bfloat16 [2, 16, 8192], P('section', 'outer', 'tensor')
- grad_sent: bfloat16 [2, 16, 8192], P('section', 'outer', 'tensor')
All inputs are finite; a program needn't handle non-finite values.
Results may differ from a plain program's by a relative error of at most 0.025.
Values may be sent and summed in bfloat16 or wider, within the bound.
A program may use at most 128 MiB of HBM per device.

v0:
```python
import functools

import jax
import jax.numpy as jnp
from jax import lax
from jax.experimental import pallas as pl
from jax.experimental.pallas import tpu as pltpu
from jax.sharding import PartitionSpec as P

MESH = pl.DeviceIdType.MESH
F32 = jnp.float32
BF16 = jnp.bfloat16
CONTRACT_LAST = (((1,), (1,)), ((), ()))
SUM_LAG = 2
SECOND_LAG = 4
AHEAD = 2


def kernel(
    sections, outers, tensors, chunks, chunk,
    act, saved, cot, w_gate, w_up, w_down,
    out_ref, grad_ref,
    gate_buf, up_buf, down_buf, gathered, staging, rows_f32, lhs_two, lhs_cot,
    products, part, arrived, shared, second_f32, total, final_out, final_in,
    load_sem, weight_sem, gather_send, gather_recv, part_send, part_recv,
    share_send, share_recv, final_send, final_recv,
):
    section = lax.axis_index("section")
    outer = lax.axis_index("outer")
    tensor = lax.axis_index("tensor")
    other = lax.rem(section + 1, sections)
    own_rows = act.shape[1]
    rows = own_rows * outers
    cells = own_rows // outers
    shard = rows // tensors

    loads = [
        pltpu.make_async_copy(source.at[0], gathered.at[which, outer], load_sem.at[which])
        for which, source in enumerate((act, saved, cot))
    ]
    for load in loads:
        load.start()

    def weight_copies(c):
        span = pl.ds(pl.multiple_of(c * chunk, chunk), chunk)
        return (
            pltpu.make_async_copy(w_gate.at[0, :, span], gate_buf.at[c], weight_sem.at[0, c]),
            pltpu.make_async_copy(w_up.at[0, :, span], up_buf.at[c], weight_sem.at[1, c]),
            pltpu.make_async_copy(w_down.at[0, span, :], down_buf.at[c], weight_sem.at[2, c]),
        )

    for c in range(min(AHEAD, chunks)):
        for copy in weight_copies(c):
            copy.start(priority=1)

    barrier = pltpu.get_barrier_semaphore()
    for step in range(1, outers):
        pl.semaphore_signal(
            barrier, 1, device_id={"outer": lax.rem(outer + step, outers)}, device_id_type=MESH
        )
    for step in range(1, tensors):
        pl.semaphore_signal(
            barrier, 1, device_id={"tensor": lax.rem(tensor + step, tensors)}, device_id_type=MESH
        )
    for place in range(outers):
        pl.semaphore_signal(
            barrier, 1, device_id={"section": other, "outer": place}, device_id_type=MESH
        )
    pl.semaphore_wait(barrier, 2 * outers + tensors - 2)

    def gather_copy(which, origin, target):
        return pltpu.make_async_remote_copy(
            src_ref=gathered.at[which, origin],
            dst_ref=gathered.at[which, origin],
            send_sem=gather_send.at[which, target],
            recv_sem=gather_recv.at[which, origin],
            device_id={"outer": target},
            device_id_type=MESH,
        )

    for which in range(3):
        loads[which].wait()
        for step in range(1, outers):
            gather_copy(which, outer, lax.rem(outer + step, outers)).start()

    for which in range(3):
        for step in range(1, outers):
            origin = lax.rem(outer + step, outers)
            gather_copy(which, origin, origin).wait_recv()
        for origin in range(outers):
            staging[...] = gathered[which, origin].astype(F32)
            for j in range(outers):
                to = (j * outers + origin) * cells
                rows_f32[which, to : to + cells, :] = staging[j * cells : (j + 1) * cells, :]
    lhs_two[0:rows, :] = rows_f32[0].astype(BF16)
    lhs_two[rows : 2 * rows, :] = rows_f32[1].astype(BF16)
    lhs_cot[...] = rows_f32[2].astype(BF16)
    place = lax.broadcasted_iota(jnp.int32, total.shape[1:], 0)
    mine = lax.rem(lax.div(place, cells), outers) == outer
    total[0] = jnp.where(mine, rows_f32[0], 0.0)
    total[1] = jnp.where(mine, rows_f32[2], 0.0)

    def part_copy(c, origin, target):
        return pltpu.make_async_remote_copy(
            src_ref=part.at[c, target],
            dst_ref=arrived.at[c, origin],
            send_sem=part_send.at[c, target],
            recv_sem=part_recv.at[c, origin],
            device_id={"tensor": target},
            device_id_type=MESH,
        )

    def share_copy(c, origin, target):
        return pltpu.make_async_remote_copy(
            src_ref=shared.at[c, origin],
            dst_ref=shared.at[c, origin],
            send_sem=share_send.at[c, target],
            recv_sem=share_recv.at[c, origin],
            device_id={"tensor": target},
            device_id_type=MESH,
        )

    def first(c):
        @pl.when(c + AHEAD < chunks)
        def _():
            for copy in weight_copies(c + AHEAD):
                copy.start(priority=1)

        for copy in weight_copies(c):
            copy.wait()
        two = lhs_two[...]
        products[0 : 2 * rows, :] = jnp.dot(two, gate_buf[c], preferred_element_type=F32)
        products[2 * rows : 4 * rows, :] = jnp.dot(two, up_buf[c], preferred_element_type=F32)
        products[4 * rows : 5 * rows, :] = lax.dot_general(
            lhs_cot[...], down_buf[c], CONTRACT_LAST, preferred_element_type=F32
        )
        for target in range(tensors):
            for which in range(5):
                part[c, target, which] = products[
                    which * rows + target * shard : which * rows + (target + 1) * shard, :
                ].astype(BF16)
        for step in range(1, tensors):
            part_copy(c, tensor, lax.rem(tensor + step, tensors)).start()

    def combine(c):
        for step in range(1, tensors):
            origin = lax.rem(tensor + step, tensors)
            part_copy(c, origin, origin).wait_recv()
        sums = []
        for which in range(5):
            summed = part[c, tensor, which].astype(F32)
            for step in range(1, tensors):
                summed = summed + arrived[c, lax.rem(tensor + step, tensors), which].astype(F32)
            sums.append(summed)
        gate_pre, gate_saved, up_pre, up_saved, hidden_grad = sums
        squash = jax.nn.sigmoid(gate_saved)
        shared[c, tensor, 0] = (gate_pre * jax.nn.sigmoid(gate_pre) * up_pre).astype(BF16)
        shared[c, tensor, 1] = (
            hidden_grad * up_saved * squash * (1.0 + gate_saved * (1.0 - squash))
        ).astype(BF16)
        shared[c, tensor, 2] = (hidden_grad * gate_saved * squash).astype(BF16)
        for step in range(1, tensors):
            share_copy(c, tensor, lax.rem(tensor + step, tensors)).start()

    def second(c):
        for step in range(1, tensors):
            origin = lax.rem(tensor + step, tensors)
            share_copy(c, origin, origin).wait_recv()
        for origin in range(tensors):
            for which in range(3):
                second_f32[which, origin * shard : (origin + 1) * shard, :] = shared[
                    c, origin, which
                ].astype(F32)
        total[0] += jnp.dot(
            second_f32[0].astype(BF16), down_buf[c], preferred_element_type=F32
        )
        total[1] += lax.dot_general(
            second_f32[1].astype(BF16), gate_buf[c], CONTRACT_LAST, preferred_element_type=F32
        ) + lax.dot_general(
            second_f32[2].astype(BF16), up_buf[c], CONTRACT_LAST, preferred_element_type=F32
        )

    def advance(step, carry):
        @pl.when(step < chunks)
        def _():
            first(step)

        @pl.when((step >= SUM_LAG) & (step < chunks + SUM_LAG))
        def _():
            combine(step - SUM_LAG)

        @pl.when(step >= SECOND_LAG)
        def _():
            second(step - SECOND_LAG)

        return carry

    lax.fori_loop(0, chunks + SECOND_LAG, advance, 0)

    def final_copy(origin, target):
        return pltpu.make_async_remote_copy(
            src_ref=final_out.at[target],
            dst_ref=final_in.at[origin],
            send_sem=final_send.at[target],
            recv_sem=final_recv.at[origin],
            device_id={"section": other, "outer": target},
            device_id_type=MESH,
        )

    for target in range(outers):
        for which in range(2):
            final_out[target, which] = total[
                which, target * own_rows : (target + 1) * own_rows, :
            ].astype(BF16)
        final_copy(outer, target).start()

    def drain(c, carry):
        for step in range(1, tensors):
            target = lax.rem(tensor + step, tensors)
            part_copy(c, tensor, target).wait_send()
            share_copy(c, tensor, target).wait_send()
        return carry

    lax.fori_loop(0, chunks, drain, 0)
    for which in range(3):
        for step in range(1, outers):
            gather_copy(which, outer, lax.rem(outer + step, outers)).wait_send()

    for origin in range(outers):
        final_copy(origin, origin).wait_recv()
    for which, result in enumerate((out_ref, grad_ref)):
        summed = final_in[0, which].astype(F32)
        for origin in range(1, outers):
            summed = summed + final_in[origin, which].astype(F32)
        result[0] = summed.astype(BF16)
    for target in range(outers):
        final_copy(outer, target).wait_send()


def solution(mesh):
    sections, outers, tensors = (mesh.shape[name] for name in ("section", "outer", "tensor"))

    def on_device(act_in, saved_in, cotangent, w_gate, w_up, w_down):
        own_rows, model_width = act_in.shape[1:]
        width = w_gate.shape[2]
        rows = own_rows * outers
        shard = rows // tensors
        chunk = next(size for size in (512, 256, 128, width) if width % size == 0)
        chunks = width // chunk
        dma = pltpu.SemaphoreType.DMA
        out = jax.ShapeDtypeStruct((1, own_rows, model_width), BF16)
        return pl.pallas_call(
            functools.partial(kernel, sections, outers, tensors, chunks, chunk),
            out_shape=(out, out),
            in_specs=[pl.BlockSpec(memory_space=pl.ANY)] * 6,
            out_specs=[pl.BlockSpec(memory_space=pltpu.VMEM)] * 2,
            scratch_shapes=[
                pltpu.VMEM((chunks, model_width, chunk), BF16),
                pltpu.VMEM((chunks, model_width, chunk), BF16),
                pltpu.VMEM((chunks, chunk, model_width), BF16),
                pltpu.VMEM((3, outers, own_rows, model_width), BF16),
                pltpu.VMEM((own_rows, model_width), F32),
                pltpu.VMEM((3, rows, model_width), F32),
                pltpu.VMEM((2 * rows, model_width), BF16),
                pltpu.VMEM((rows, model_width), BF16),
                pltpu.VMEM((5 * rows, chunk), F32),
                pltpu.VMEM((chunks, tensors, 5, shard, chunk), BF16),
                pltpu.VMEM((chunks, tensors, 5, shard, chunk), BF16),
                pltpu.VMEM((chunks, tensors, 3, shard, chunk), BF16),
                pltpu.VMEM((3, rows, chunk), F32),
                pltpu.VMEM((2, rows, model_width), F32),
                pltpu.VMEM((outers, 2, own_rows, model_width), BF16),
                pltpu.VMEM((outers, 2, own_rows, model_width), BF16),
                dma((3,)),
                dma((3, chunks)),
                dma((3, outers)),
                dma((3, outers)),
                dma((chunks, tensors)),
                dma((chunks, tensors)),
                dma((chunks, tensors)),
                dma((chunks, tensors)),
                dma((outers,)),
                dma((outers,)),
            ],
            compiler_params=pltpu.CompilerParams(
                collective_id=0, has_side_effects=True, vmem_limit_bytes=60 * 1024 * 1024
            ),
        )(act_in, saved_in, cotangent, w_gate, w_up, w_down)

    return jax.shard_map(
        on_device,
        mesh=mesh,
        in_specs=(
            P("section", "outer", "tensor"),
            P("section", "outer", "tensor"),
            P("section", "outer", "tensor"),
            P("section", "tensor", "outer"),
            P("section", "tensor", "outer"),
            P("section", "outer", "tensor"),
        ),
        out_specs=(P("section", "outer", "tensor"), P("section", "outer", "tensor")),
        check_vma=False,
    )
```

profile of v0, /device:TPU:0, one launch (start us, length us, event | category | flops | bytes accessed | tf_op | source)
XLA Modules:
  0.0 44.6 jit_solution(5664619925211248216)
XLA Ops:
  0.6 41.3 %shard_map.77 = (bf16[1,4,2048]{2,1,0:T(4,128)(2,1)}, bf16[1,4,2048]{2,1,0:T(4,128)(2,1)}) custom-call(bf16[1,4,2048]{2,1,0:T(4,128)(2,1)} %act.1, bf16[1,4,2048]{2,1,0:T(4,128)(2,1)} %saved.1, bf16[1,4,2048]{2,1,0:T(4,128)(2,1)} %cot.1, bf16[1,2048,3584]{2,1,0:T(8,128)(2,1)} %w_gate.1, bf16[1,2048,3584]{2,1,0:T(8,128)(2,1)} %w_up.1, ...), custom_call_target="tpu_custom_call" | custom-call | tf_op jit(solution)/shard_map/pallas_call | solution.py:252
  41.9 1.3 %copy.10 = bf16[1,4,2048]{2,1,0:T(4,128)(2,1)} copy(bf16[1,4,2048]{2,1,0:T(4,128)(2,1)} %get-tuple-element.4) | data formatting | bytes 32768
  43.3 1.3 %copy.11 = bf16[1,4,2048]{2,1,0:T(4,128)(2,1)} copy(bf16[1,4,2048]{2,1,0:T(4,128)(2,1)} %get-tuple-element.5) | data formatting | bytes 32768
where the time goes:
time: 44.9 us; the launch traced here: 44.6 us
  Pallas kernels  41.3 us (92%)
  local copies, waits for them, and re-layouts  2.66 us (6%)
  between operations  0.64 us (1%)
    pallas_call x1, Pallas kernels, on_device(): pl.pallas_call(functools.partial(kernel, sections, outers, tensors, chunk...  41.3 us
    unnamed x2, local copies, waits for them, and re-layouts  2.66 us

commit v1 on v0

--- a/solution.py
+++ b/solution.py
@@ -14,6 +14,9 @@
 SUM_LAG = 2
 SECOND_LAG = 4
 AHEAD = 2
+SUM_AFTER = 3
+SECOND_AFTER = 5
+PAIRED = 0
 
 
 def kernel(
@@ -237,6 +240,312 @@
         final_copy(outer, target).wait_send()
 
 
+def fast_kernel(
+    outers, tensors, chunks, chunk, paired,
+    act, saved, cot, w_gate, w_up, w_down,
+    out_ref,
+    gate_buf, up_buf, down_buf, up_turned, gathered, rows_f32, lhs_two, lhs_cot,
+    part, arrived, passed, joined, shared, total, final_out, final_in,
+    load_sem, weight_sem, gather_send, gather_recv, part_send, part_recv, pass_recv,
+    share_send, share_recv, final_send, final_recv,
+):
+    section = lax.axis_index("section")
+    outer = lax.axis_index("outer")
+    tensor = lax.axis_index("tensor")
+    other = 1 - section
+    own_rows = act.shape[1]
+    rows = own_rows * outers
+    lanes = chunk // tensors
+    left = tensor < 2
+    is_end = (tensor == 0) | (tensor == 3)
+    partner = tensor + 1 - 2 * lax.rem(tensor, 2)
+    far_inner = jnp.where(left, 2, 1)
+    far_end = jnp.where(left, 3, 0)
+    fars = (far_inner, far_end)
+    peers = [lax.rem(tensor + step, tensors) for step in range(1, tensors)]
+
+    loads = [
+        pltpu.make_async_copy(source.at[0], gathered.at[which, outer], load_sem.at[which])
+        for which, source in enumerate((act, saved, cot))
+    ]
+    for load in loads:
+        load.start()
+    weight_copies = []
+    for c in range(chunks):
+        span = pl.ds(c * chunk, chunk)
+        copies = (
+            pltpu.make_async_copy(w_gate.at[0, :, span], gate_buf.at[c], weight_sem.at[0, c]),
+            pltpu.make_async_copy(w_up.at[0, :, span], up_buf.at[c], weight_sem.at[1, c]),
+            pltpu.make_async_copy(w_down.at[0, span, :], down_buf.at[c], weight_sem.at[2, c]),
+        )
+        for copy in copies:
+            copy.start(priority=1)
+        weight_copies.append(copies)
+
+    barrier = pltpu.get_barrier_semaphore()
+    for step in range(1, outers):
+        pl.semaphore_signal(
+            barrier, 1, device_id={"outer": lax.rem(outer + step, outers)}, device_id_type=MESH
+        )
+    for peer in peers:
+        pl.semaphore_signal(barrier, 1, device_id={"tensor": peer}, device_id_type=MESH)
+    for place in range(outers):
+        pl.semaphore_signal(
+            barrier, 1, device_id={"section": other, "outer": place}, device_id_type=MESH
+        )
+    for load in loads:
+        load.wait()
+    pl.semaphore_wait(barrier, 2 * outers + tensors - 2)
+
+    def gather_copy(which, origin, target):
+        return pltpu.make_async_remote_copy(
+            src_ref=gathered.at[which, origin],
+            dst_ref=gathered.at[which, origin],
+            send_sem=gather_send.at[which, target],
+            recv_sem=gather_recv.at[which, origin],
+            device_id={"outer": target},
+            device_id_type=MESH,
+        )
+
+    for which in range(3):
+        for step in range(1, outers):
+            gather_copy(which, outer, lax.rem(outer + step, outers)).start()
+    for which in range(3):
+        for step in range(1, outers):
+            origin = lax.rem(outer + step, outers)
+            gather_copy(which, origin, origin).wait_recv()
+        for origin in range(outers):
+            rows_f32[which, origin * own_rows : (origin + 1) * own_rows, :] = gathered[
+                which, origin
+            ].astype(F32)
+    row = lax.broadcasted_iota(jnp.int32, (rows, rows), 0)
+    column = lax.broadcasted_iota(jnp.int32, (rows, rows), 1)
+    takes = lax.rem(row, outers) * own_rows + lax.div(row, outers) == column
+    turn = jnp.where(takes, 1.0, 0.0).astype(BF16)
+    ordered = [
+        jnp.dot(turn, rows_f32[which].astype(BF16), preferred_element_type=F32)
+        for which in range(3)
+    ]
+    lhs_two[0:rows, :] = ordered[0].astype(BF16)
+    lhs_two[rows : 2 * rows, :] = ordered[1].astype(BF16)
+    lhs_cot[...] = ordered[2].astype(BF16)
+    place = lax.broadcasted_iota(jnp.int32, total.shape[1:], 0)
+    mine = lax.rem(place, outers) == outer
+    total[0] = jnp.where(mine, ordered[0], 0.0)
+    total[1] = jnp.where(mine, ordered[2], 0.0)
+
+    def part_copy(c, source, origin, target):
+        return pltpu.make_async_remote_copy(
+            src_ref=source,
+            dst_ref=arrived.at[c, origin],
+            send_sem=part_send.at[c, target],
+            recv_sem=part_recv.at[c, origin],
+            device_id={"tensor": target},
+            device_id_type=MESH,
+        )
+
+    def pass_copy(c, k, far):
+        return pltpu.make_async_remote_copy(
+            src_ref=part.at[c, far],
+            dst_ref=passed.at[c, k],
+            send_sem=part_send.at[c, far],
+            recv_sem=pass_recv.at[c, k],
+            device_id={"tensor": partner},
+            device_id_type=MESH,
+        )
+
+    def share_copy(c, origin, target):
+        return pltpu.make_async_remote_copy(
+            src_ref=shared.at[c, origin],
+            dst_ref=shared.at[c, origin],
+            send_sem=share_send.at[c, target],
+            recv_sem=share_recv.at[c, origin],
+            device_id={"tensor": target},
+            device_id_type=MESH,
+        )
+
+    def first(c):
+        for copy in weight_copies[c]:
+            copy.wait()
+        gate = jnp.dot(lhs_two[...], gate_buf[c], preferred_element_type=F32)
+        up = jnp.dot(lhs_two[...], up_buf[c], preferred_element_type=F32)
+        grad = lax.dot_general(lhs_cot[...], down_buf[c], CONTRACT_LAST, preferred_element_type=F32)
+        for target in range(tensors):
+            span = slice(target * lanes, (target + 1) * lanes)
+            part[c, target, 0 : 2 * rows] = gate[:, span].astype(BF16)
+            part[c, target, 2 * rows : 4 * rows] = up[:, span].astype(BF16)
+            part[c, target, 4 * rows : 5 * rows] = grad[:, span].astype(BF16)
+        if c < paired:
+            @pl.when(is_end)
+            def _():
+                for k, far in enumerate(fars):
+                    pass_copy(c, k, far).start()
+
+            part_copy(c, part.at[c, partner], tensor, partner).start()
+        else:
+            for peer in peers:
+                part_copy(c, part.at[c, peer], tensor, peer).start()
+        up_turned[c] = up_buf[c].T
+
+    def relay(c):
+        if c >= paired:
+            return
+
+        @pl.when(jnp.logical_not(is_end))
+        def _():
+            for k, far in enumerate(fars):
+                pass_copy(c, k, far).wait_recv()
+                joined[c, k] = (part[c, far].astype(F32) + passed[c, k].astype(F32)).astype(BF16)
+                part_copy(c, joined.at[c, k], tensor, far).start()
+
+    def combine(c):
+        origins = [partner, far_inner] if c < paired else peers
+        for origin in origins:
+            part_copy(c, part.at[c, origin], origin, origin).wait_recv()
+        summed = part[c, tensor].astype(F32)
+        for origin in origins:
+            summed = summed + arrived[c, origin].astype(F32)
+        gate_pre, gate_saved, up_pre, up_saved, hidden_grad = (
+            summed[which * rows : (which + 1) * rows] for which in range(5)
+        )
+        squash = jax.nn.sigmoid(gate_saved)
+        shared[c, tensor, 0:rows] = (gate_pre * jax.nn.sigmoid(gate_pre) * up_pre).astype(BF16)
+        shared[c, tensor, rows : 2 * rows] = (
+            hidden_grad * up_saved * squash * (1.0 + gate_saved * (1.0 - squash))
+        ).astype(BF16)
+        shared[c, tensor, 2 * rows : 3 * rows] = (hidden_grad * gate_saved * squash).astype(BF16)
+        for peer in peers:
+            share_copy(c, tensor, peer).start()
+
+    def final_copy(which, origin, target):
+        return pltpu.make_async_remote_copy(
+            src_ref=final_out.at[which, target],
+            dst_ref=final_in.at[which, origin],
+            send_sem=final_send.at[which, target],
+            recv_sem=final_recv.at[which, origin],
+            device_id={"section": other, "outer": target},
+            device_id_type=MESH,
+        )
+
+    def send_final(which):
+        for target in range(outers):
+            final_out[which, target] = total[
+                which, target * own_rows : (target + 1) * own_rows, :
+            ].astype(BF16)
+            final_copy(which, outer, target).start()
+
+    def second(c):
+        for peer in peers:
+            share_copy(c, peer, peer).wait_recv()
+
+        def side(which):
+            return jnp.concatenate(
+                [shared[c, t, which * rows : (which + 1) * rows] for t in range(tensors)], axis=1
+            )
+
+        total[0] += jnp.dot(side(0), down_buf[c], preferred_element_type=F32)
+        if c == chunks - 1:
+            send_final(0)
+        total[1] += lax.dot_general(
+            side(1), gate_buf[c], CONTRACT_LAST, preferred_element_type=F32
+        ) + jnp.dot(side(2), up_turned[c], preferred_element_type=F32)
+
+    last = chunks - 1
+    for step in range(chunks):
+        first(step)
+        if step >= 1:
+            relay(step - 1)
+        if step >= SUM_AFTER:
+            combine(step - SUM_AFTER)
+        if step >= SECOND_AFTER:
+            second(step - SECOND_AFTER)
+    done = max(chunks - SECOND_AFTER, 0)
+    for c in range(max(chunks - SUM_AFTER, 0), chunks):
+        combine(c) if c < last else relay(c)
+        if c < last and done < c:
+            second(done)
+            done += 1
+    combine(last)
+    while done < chunks:
+        second(done)
+        done += 1
+    send_final(1)
+
+    def drain(c, carry):
+        for peer in peers:
+            part_copy(c, part.at[c, peer], tensor, peer).wait_send()
+            share_copy(c, tensor, peer).wait_send()
+        return carry
+
+    lax.fori_loop(0, chunks, drain, 0)
+    for which in range(3):
+        for step in range(1, outers):
+            gather_copy(which, outer, lax.rem(outer + step, outers)).wait_send()
+    for which in range(2):
+        for origin in range(outers):
+            final_copy(which, origin, origin).wait_recv()
+        summed = final_in[which, 0].astype(F32)
+        for origin in range(1, outers):
+            summed = summed + final_in[which, origin].astype(F32)
+        out_ref[which] = summed.astype(BF16)
+    for which in range(2):
+        for target in range(outers):
+            final_copy(which, outer, target).wait_send()
+
+
+def part_out(both, out_ref, grad_ref):
+    out_ref[0] = both[0]
+    grad_ref[0] = both[1]
+
+
+def fast_call(outers, tensors, chunk, act_in, saved_in, cotangent, w_gate, w_up, w_down):
+    own_rows, model_width = act_in.shape[1:]
+    chunks = w_gate.shape[2] // chunk
+    rows = own_rows * outers
+    lanes = chunk // tensors
+    dma = pltpu.SemaphoreType.DMA
+    both = pl.pallas_call(
+        functools.partial(fast_kernel, outers, tensors, chunks, chunk, PAIRED),
+        out_shape=jax.ShapeDtypeStruct((2, own_rows, model_width), BF16),
+        in_specs=[pl.BlockSpec(memory_space=pl.ANY)] * 6,
+        out_specs=pl.BlockSpec(memory_space=pltpu.VMEM),
+        scratch_shapes=[
+            pltpu.VMEM((chunks, model_width, chunk), BF16),
+            pltpu.VMEM((chunks, model_width, chunk), BF16),
+            pltpu.VMEM((chunks, chunk, model_width), BF16),
+            pltpu.VMEM((chunks, chunk, model_width), BF16),
+            pltpu.VMEM((3, outers, own_rows, model_width), BF16),
+            pltpu.VMEM((3, rows, model_width), F32),
+            pltpu.VMEM((2 * rows, model_width), BF16),
+            pltpu.VMEM((rows, model_width), BF16),
+            pltpu.VMEM((chunks, tensors, 5 * rows, lanes), BF16),
+            pltpu.VMEM((chunks, tensors, 5 * rows, lanes), BF16),
+            pltpu.VMEM((chunks, 2, 5 * rows, lanes), BF16),
+            pltpu.VMEM((chunks, 2, 5 * rows, lanes), BF16),
+            pltpu.VMEM((chunks, tensors, 3 * rows, lanes), BF16),
+            pltpu.VMEM((2, rows, model_width), F32),
+            pltpu.VMEM((2, outers, own_rows, model_width), BF16),
+            pltpu.VMEM((2, outers, own_rows, model_width), BF16),
+            dma((3,)),
+            dma((3, chunks)),
+            dma((3, outers)),
+            dma((3, outers)),
+            dma((chunks, tensors)),
+            dma((chunks, tensors)),
+            dma((chunks, 2)),
+            dma((chunks, tensors)),
+            dma((chunks, tensors)),
+            dma((2, outers)),
+            dma((2, outers)),
+        ],
+        compiler_params=pltpu.CompilerParams(
+            collective_id=0, has_side_effects=True, vmem_limit_bytes=63 * 1024 * 1024
+        ),
+    )(act_in, saved_in, cotangent, w_gate, w_up, w_down)
+    out = jax.ShapeDtypeStruct((1, own_rows, model_width), BF16)
+    return pl.pallas_call(part_out, out_shape=(out, out))(both)
+
+
 def solution(mesh):
     sections, outers, tensors = (mesh.shape[name] for name in ("section", "outer", "tensor"))
 
@@ -244,6 +553,11 @@
         own_rows, model_width = act_in.shape[1:]
         width = w_gate.shape[2]
         rows = own_rows * outers
+        if sections == 2 and tensors == 4 and own_rows == outers and rows % 16 == 0 and width % 512 == 0:
+            if 4 * width * model_width * 2 <= 56 * 1024 * 1024:
+                return fast_call(
+                    outers, tensors, 512, act_in, saved_in, cotangent, w_gate, w_up, w_down
+                )
         shard = rows // tensors
         chunk = next(size for size in (512, 256, 128, width) if width % size == 0)
         chunks = width // chunk

time: 44.9 us -> 44.8 us (level)
  local copies, waits for them, and re-layouts: 2.66 us -> 0 us
  Pallas kernels: 41.3 us -> 43.9 us
    unnamed x2 -> x0, local copies, waits for them, and re-layouts: 2.66 us -> none
    pallas_call x1 -> x2, Pallas kernels: 41.3 us -> 43.9 us  [the longest x1 42.6 us: fast_call(): pl.pallas_call(functools.partial(fast_kernel, outers, tensors, chunks, ch...]
where the time goes in v1:
time: 44.8 us; the launch traced here: 44.6 us
  Pallas kernels  43.9 us (98%)
  between operations  0.64 us (1%)
    pallas_call x1, Pallas kernels, fast_call(): pl.pallas_call(functools.partial(fast_kernel, outers, tensors, chunks, ch...  42.6 us
    pallas_call x1, Pallas kernels, fast_call(): return pl.pallas_call(part_out, out_shape=(out, out))(both)  1.37 us

profile of v1, /device:TPU:0, one launch (start us, length us, event | category | flops | bytes accessed | tf_op | source)
XLA Modules:
  0.0 44.6 jit_solution(15755350857481780841)
XLA Ops:
  0.6 42.6 %shard_map.77.both = bf16[2,4,2048]{2,1,0:T(4,128)(2,1)} custom-call(bf16[1,4,2048]{2,1,0:T(4,128)(2,1)} %act.1, bf16[1,4,2048]{2,1,0:T(4,128)(2,1)} %saved.1, bf16[1,4,2048]{2,1,0:T(4,128)(2,1)} %cot.1, bf16[1,2048,3584]{2,1,0:T(8,128)(2,1)} %w_gate.1, bf16[1,2048,3584]{2,1,0:T(8,128)(2,1)} %w_up.1, bf16[1,3584,2048]{2,1,0:T(8,128)(2,1)} %w_down.1), custom_call_target="tpu_custom_call" | custom-call | tf_op jit(solution)/shard_map/pallas_call | solution.py:507
  43.2 1.4 %shard_map.78 = (bf16[1,4,2048]{2,1,0:T(4,128)(2,1)}, bf16[1,4,2048]{2,1,0:T(4,128)(2,1)}) custom-call(bf16[2,4,2048]{2,1,0:T(4,128)(2,1)} %shard_map.77.both), custom_call_target="tpu_custom_call" | custom-call | tf_op jit(solution)/shard_map/pallas_call | solution.py:546

commit v2 on v1

--- a/solution.py
+++ b/solution.py
@@ -14,9 +14,12 @@
 SUM_LAG = 2
 SECOND_LAG = 4
 AHEAD = 2
-SUM_AFTER = 3
-SECOND_AFTER = 5
-PAIRED = 0
+RELAY_AFTER = 2
+SUM_AFTER = 4
+DIRECT_AFTER = 3
+SECOND_AFTER = 6
+DIRECT_FIRST = 2
+DIRECT_LAST = 0
 
 
 def kernel(
@@ -255,13 +258,14 @@
     other = 1 - section
     own_rows = act.shape[1]
     rows = own_rows * outers
-    lanes = chunk // tensors
+    lanes = chunk // 2
     left = tensor < 2
     is_end = (tensor == 0) | (tensor == 3)
-    partner = tensor + 1 - 2 * lax.rem(tensor, 2)
-    far_inner = jnp.where(left, 2, 1)
-    far_end = jnp.where(left, 3, 0)
-    fars = (far_inner, far_end)
+    is_inner = jnp.logical_not(is_end)
+    inner, end = jnp.where(left, 1, 2), jnp.where(left, 0, 3)
+    far_inner, far_end = 3 - inner, 3 - end
+    mine_half = jnp.where(left, 0, 1)
+    far_half = 1 - mine_half
     peers = [lax.rem(tensor + step, tensors) for step in range(1, tensors)]
 
     loads = [
@@ -270,6 +274,17 @@
     ]
     for load in loads:
         load.start()
+    barrier = pltpu.get_barrier_semaphore()
+    for step in range(1, outers):
+        pl.semaphore_signal(
+            barrier, 1, device_id={"outer": lax.rem(outer + step, outers)}, device_id_type=MESH
+        )
+    for peer in peers:
+        pl.semaphore_signal(barrier, 1, device_id={"tensor": peer}, device_id_type=MESH)
+    for place in range(outers):
+        pl.semaphore_signal(
+            barrier, 1, device_id={"section": other, "outer": place}, device_id_type=MESH
+        )
     weight_copies = []
     for c in range(chunks):
         span = pl.ds(c * chunk, chunk)
@@ -282,17 +297,6 @@
             copy.start(priority=1)
         weight_copies.append(copies)
 
-    barrier = pltpu.get_barrier_semaphore()
-    for step in range(1, outers):
-        pl.semaphore_signal(
-            barrier, 1, device_id={"outer": lax.rem(outer + step, outers)}, device_id_type=MESH
-        )
-    for peer in peers:
-        pl.semaphore_signal(barrier, 1, device_id={"tensor": peer}, device_id_type=MESH)
-    for place in range(outers):
-        pl.semaphore_signal(
-            barrier, 1, device_id={"section": other, "outer": place}, device_id_type=MESH
-        )
     for load in loads:
         load.wait()
     pl.semaphore_wait(barrier, 2 * outers + tensors - 2)
@@ -334,35 +338,52 @@
     total[0] = jnp.where(mine, ordered[0], 0.0)
     total[1] = jnp.where(mine, ordered[2], 0.0)
 
-    def part_copy(c, source, origin, target):
+    def part_copy(c, source, slot, lane, target):
         return pltpu.make_async_remote_copy(
             src_ref=source,
-            dst_ref=arrived.at[c, origin],
-            send_sem=part_send.at[c, target],
-            recv_sem=part_recv.at[c, origin],
+            dst_ref=arrived.at[c, slot],
+            send_sem=part_send.at[c, lane],
+            recv_sem=part_recv.at[c, slot],
             device_id={"tensor": target},
             device_id_type=MESH,
         )
 
-    def pass_copy(c, k, far):
-        return pltpu.make_async_remote_copy(
-            src_ref=part.at[c, far],
-            dst_ref=passed.at[c, k],
-            send_sem=part_send.at[c, far],
-            recv_sem=pass_recv.at[c, k],
-            device_id={"tensor": partner},
-            device_id_type=MESH,
-        )
-
-    def share_copy(c, origin, target):
-        return pltpu.make_async_remote_copy(
-            src_ref=shared.at[c, origin],
-            dst_ref=shared.at[c, origin],
-            send_sem=share_send.at[c, target],
-            recv_sem=share_recv.at[c, origin],
+    def pass_copy(c):
+        return pltpu.make_async_remote_copy(
+            src_ref=part.at[c, far_half],
+            dst_ref=passed.at[c],
+            send_sem=part_send.at[c, 0],
+            recv_sem=pass_recv.at[c],
+            device_id={"tensor": inner},
+            device_id_type=MESH,
+        )
+
+    def share_copy(c, half, lane, target):
+        return pltpu.make_async_remote_copy(
+            src_ref=shared.at[c, half],
+            dst_ref=shared.at[c, half],
+            send_sem=share_send.at[c, lane],
+            recv_sem=share_recv.at[c, half],
             device_id={"tensor": target},
             device_id_type=MESH,
         )
+
+    def end_sends(c):
+        if c in paired:
+            across = pass_copy(c)
+        else:
+            across = part_copy(c, part.at[c, far_half], 1, 0, far_inner)
+        return across, part_copy(c, part.at[c, mine_half], 0, 1, inner)
+
+    def inner_send(c):
+        source = joined.at[c] if c in paired else part.at[c, far_half]
+        return part_copy(c, source, 2, 0, far_inner)
+
+    def share_sends(c):
+        return [
+            share_copy(c, mine_half, lane, target)
+            for lane, target in enumerate((far_inner, far_end, end))
+        ]
 
     def first(c):
         for copy in weight_copies[c]:
@@ -370,52 +391,50 @@
         gate = jnp.dot(lhs_two[...], gate_buf[c], preferred_element_type=F32)
         up = jnp.dot(lhs_two[...], up_buf[c], preferred_element_type=F32)
         grad = lax.dot_general(lhs_cot[...], down_buf[c], CONTRACT_LAST, preferred_element_type=F32)
-        for target in range(tensors):
-            span = slice(target * lanes, (target + 1) * lanes)
-            part[c, target, 0 : 2 * rows] = gate[:, span].astype(BF16)
-            part[c, target, 2 * rows : 4 * rows] = up[:, span].astype(BF16)
-            part[c, target, 4 * rows : 5 * rows] = grad[:, span].astype(BF16)
-        if c < paired:
-            @pl.when(is_end)
+        up_turned[c] = up_buf[c].T
+        for half in range(2):
+            span = slice(half * lanes, (half + 1) * lanes)
+            part[c, half, 0 : 2 * rows] = gate[:, span].astype(BF16)
+            part[c, half, 2 * rows : 4 * rows] = up[:, span].astype(BF16)
+            part[c, half, 4 * rows : 5 * rows] = grad[:, span].astype(BF16)
+
+        @pl.when(is_end)
+        def _():
+            for copy in end_sends(c):
+                copy.start()
+
+        if c not in paired:
+            @pl.when(is_inner)
             def _():
-                for k, far in enumerate(fars):
-                    pass_copy(c, k, far).start()
-
-            part_copy(c, part.at[c, partner], tensor, partner).start()
-        else:
-            for peer in peers:
-                part_copy(c, part.at[c, peer], tensor, peer).start()
-        up_turned[c] = up_buf[c].T
+                inner_send(c).start()
 
     def relay(c):
-        if c >= paired:
-            return
-
-        @pl.when(jnp.logical_not(is_end))
-        def _():
-            for k, far in enumerate(fars):
-                pass_copy(c, k, far).wait_recv()
-                joined[c, k] = (part[c, far].astype(F32) + passed[c, k].astype(F32)).astype(BF16)
-                part_copy(c, joined.at[c, k], tensor, far).start()
+        @pl.when(is_inner)
+        def _():
+            pass_copy(c).wait_recv()
+            joined[c] = (part[c, far_half].astype(F32) + passed[c].astype(F32)).astype(BF16)
+            inner_send(c).start()
 
     def combine(c):
-        origins = [partner, far_inner] if c < paired else peers
-        for origin in origins:
-            part_copy(c, part.at[c, origin], origin, origin).wait_recv()
-        summed = part[c, tensor].astype(F32)
-        for origin in origins:
-            summed = summed + arrived[c, origin].astype(F32)
-        gate_pre, gate_saved, up_pre, up_saved, hidden_grad = (
-            summed[which * rows : (which + 1) * rows] for which in range(5)
-        )
-        squash = jax.nn.sigmoid(gate_saved)
-        shared[c, tensor, 0:rows] = (gate_pre * jax.nn.sigmoid(gate_pre) * up_pre).astype(BF16)
-        shared[c, tensor, rows : 2 * rows] = (
-            hidden_grad * up_saved * squash * (1.0 + gate_saved * (1.0 - squash))
-        ).astype(BF16)
-        shared[c, tensor, 2 * rows : 3 * rows] = (hidden_grad * gate_saved * squash).astype(BF16)
-        for peer in peers:
-            share_copy(c, tensor, peer).start()
+        @pl.when(is_inner)
+        def _():
+            slots = (0, 2) if c in paired else (0, 1, 2)
+            for slot in slots:
+                part_copy(c, part.at[c, 0], slot, 0, inner).wait_recv()
+            summed = part[c, mine_half].astype(F32)
+            for slot in slots:
+                summed = summed + arrived[c, slot].astype(F32)
+            gate_pre, gate_saved, up_pre, up_saved, hidden_grad = (
+                summed[which * rows : (which + 1) * rows] for which in range(5)
+            )
+            squash = jax.nn.sigmoid(gate_saved)
+            forward = gate_pre * jax.nn.sigmoid(gate_pre) * up_pre
+            gate_grad = hidden_grad * up_saved * squash * (1.0 + gate_saved * (1.0 - squash))
+            up_grad = hidden_grad * gate_saved * squash
+            for which, value in enumerate((forward, gate_grad, up_grad)):
+                shared[c, mine_half, which * rows : (which + 1) * rows] = value.astype(BF16)
+            for copy in share_sends(c):
+                copy.start()
 
     def final_copy(which, origin, target):
         return pltpu.make_async_remote_copy(
@@ -435,12 +454,15 @@
             final_copy(which, outer, target).start()
 
     def second(c):
-        for peer in peers:
-            share_copy(c, peer, peer).wait_recv()
+        @pl.when(is_end)
+        def _():
+            share_copy(c, mine_half, 0, inner).wait_recv()
+
+        share_copy(c, far_half, 0, inner).wait_recv()
 
         def side(which):
             return jnp.concatenate(
-                [shared[c, t, which * rows : (which + 1) * rows] for t in range(tensors)], axis=1
+                [shared[c, half, which * rows : (which + 1) * rows] for half in range(2)], axis=1
             )
 
         total[0] += jnp.dot(side(0), down_buf[c], preferred_element_type=F32)
@@ -450,34 +472,30 @@
             side(1), gate_buf[c], CONTRACT_LAST, preferred_element_type=F32
         ) + jnp.dot(side(2), up_turned[c], preferred_element_type=F32)
 
-    last = chunks - 1
-    for step in range(chunks):
-        first(step)
-        if step >= 1:
-            relay(step - 1)
-        if step >= SUM_AFTER:
-            combine(step - SUM_AFTER)
-        if step >= SECOND_AFTER:
-            second(step - SECOND_AFTER)
-    done = max(chunks - SECOND_AFTER, 0)
-    for c in range(max(chunks - SUM_AFTER, 0), chunks):
-        combine(c) if c < last else relay(c)
-        if c < last and done < c:
-            second(done)
-            done += 1
-    combine(last)
-    while done < chunks:
-        second(done)
-        done += 1
+    steps = []
+    for c in range(chunks):
+        steps.append((c, first, c))
+        if c in paired:
+            steps.append((c + RELAY_AFTER + 0.1, relay, c))
+        steps.append((c + (SUM_AFTER if c in paired else DIRECT_AFTER) + 0.2, combine, c))
+        steps.append((c + SECOND_AFTER + 0.3, second, c))
+    for _, act_on, c in sorted(steps, key=lambda entry: entry[0]):
+        act_on(c)
     send_final(1)
 
-    def drain(c, carry):
-        for peer in peers:
-            part_copy(c, part.at[c, peer], tensor, peer).wait_send()
-            share_copy(c, tensor, peer).wait_send()
-        return carry
-
-    lax.fori_loop(0, chunks, drain, 0)
+    @pl.when(is_end)
+    def _():
+        for c in range(chunks):
+            for copy in end_sends(c):
+                copy.wait_send()
+
+    @pl.when(is_inner)
+    def _():
+        for c in range(chunks):
+            inner_send(c).wait_send()
+            for copy in share_sends(c):
+                copy.wait_send()
+
     for which in range(3):
         for step in range(1, outers):
             gather_copy(which, outer, lax.rem(outer + step, outers)).wait_send()
@@ -502,10 +520,12 @@
     own_rows, model_width = act_in.shape[1:]
     chunks = w_gate.shape[2] // chunk
     rows = own_rows * outers
-    lanes = chunk // tensors
+    lanes = chunk // 2
     dma = pltpu.SemaphoreType.DMA
     both = pl.pallas_call(
-        functools.partial(fast_kernel, outers, tensors, chunks, chunk, PAIRED),
+        functools.partial(
+            fast_kernel, outers, tensors, chunks, chunk, range(DIRECT_FIRST, chunks - DIRECT_LAST)
+        ),
         out_shape=jax.ShapeDtypeStruct((2, own_rows, model_width), BF16),
         in_specs=[pl.BlockSpec(memory_space=pl.ANY)] * 6,
         out_specs=pl.BlockSpec(memory_space=pltpu.VMEM),
@@ -518,11 +538,11 @@
             pltpu.VMEM((3, rows, model_width), F32),
             pltpu.VMEM((2 * rows, model_width), BF16),
             pltpu.VMEM((rows, model_width), BF16),
-            pltpu.VMEM((chunks, tensors, 5 * rows, lanes), BF16),
-            pltpu.VMEM((chunks, tensors, 5 * rows, lanes), BF16),
             pltpu.VMEM((chunks, 2, 5 * rows, lanes), BF16),
-            pltpu.VMEM((chunks, 2, 5 * rows, lanes), BF16),
-            pltpu.VMEM((chunks, tensors, 3 * rows, lanes), BF16),
+            pltpu.VMEM((chunks, 3, 5 * rows, lanes), BF16),
+            pltpu.VMEM((chunks, 5 * rows, lanes), BF16),
+            pltpu.VMEM((chunks, 5 * rows, lanes), BF16),
+            pltpu.VMEM((chunks, 2, 3 * rows, lanes), BF16),
             pltpu.VMEM((2, rows, model_width), F32),
             pltpu.VMEM((2, outers, own_rows, model_width), BF16),
             pltpu.VMEM((2, outers, own_rows, model_width), BF16),
@@ -530,11 +550,11 @@
             dma((3, chunks)),
             dma((3, outers)),
             dma((3, outers)),
-            dma((chunks, tensors)),
-            dma((chunks, tensors)),
             dma((chunks, 2)),
-            dma((chunks, tensors)),
-            dma((chunks, tensors)),
+            dma((chunks, 3)),
+            dma((chunks,)),
+            dma((chunks, 3)),
+            dma((chunks, 2)),
             dma((2, outers)),
             dma((2, outers)),
         ],

time: 44.8 us -> 40.3 us (0.90)
  Pallas kernels: 43.9 us -> 39.4 us
    pallas_call x1, Pallas kernels: 42.6 us -> 38 us  [fast_call(): pl.pallas_call(functools.partial(fast_kernel, outers, tensors, chunks, ch...]
where the time goes in v2:
time: 40.3 us; the launch traced here: 40.1 us
  Pallas kernels  39.4 us (98%)
  between operations  0.64 us (2%)
    pallas_call x1, Pallas kernels, fast_call(): pl.pallas_call(functools.partial(fast_kernel, outers, tensors, chunks, ch...  38 us
    pallas_call x1, Pallas kernels, fast_call(): return pl.pallas_call(part_out, out_shape=(out, out))(both)  1.37 us

profile of v2, /device:TPU:0, one launch (start us, length us, event | category | flops | bytes accessed | tf_op | source)
XLA Modules:
  0.0 40.1 jit_solution(8164425490600211353)
XLA Ops:
  0.6 38.0 %shard_map.77.both = bf16[2,4,2048]{2,1,0:T(4,128)(2,1)} custom-call(bf16[1,4,2048]{2,1,0:T(4,128)(2,1)} %act.1, bf16[1,4,2048]{2,1,0:T(4,128)(2,1)} %saved.1, bf16[1,4,2048]{2,1,0:T(4,128)(2,1)} %cot.1, bf16[1,2048,3584]{2,1,0:T(8,128)(2,1)} %w_gate.1, bf16[1,2048,3584]{2,1,0:T(8,128)(2,1)} %w_up.1, bf16[1,3584,2048]{2,1,0:T(8,128)(2,1)} %w_down.1), custom_call_target="tpu_custom_call" | custom-call | tf_op jit(solution)/shard_map/pallas_call | solution.py:525
  38.7 1.4 %shard_map.78 = (bf16[1,4,2048]{2,1,0:T(4,128)(2,1)}, bf16[1,4,2048]{2,1,0:T(4,128)(2,1)}) custom-call(bf16[2,4,2048]{2,1,0:T(4,128)(2,1)} %shard_map.77.both), custom_call_target="tpu_custom_call" | custom-call | tf_op jit(solution)/shard_map/pallas_call | solution.py:566

commit v3 on v2

--- a/solution.py
+++ b/solution.py
@@ -248,9 +248,9 @@
     act, saved, cot, w_gate, w_up, w_down,
     out_ref,
     gate_buf, up_buf, down_buf, up_turned, gathered, rows_f32, lhs_two, lhs_cot,
-    part, arrived, passed, joined, shared, total, final_out, final_in,
+    part, arrived, passed, joined, shared, total, final_out, final_in, result,
     load_sem, weight_sem, gather_send, gather_recv, part_send, part_recv, pass_recv,
-    share_send, share_recv, final_send, final_recv,
+    share_send, share_recv, final_send, final_recv, result_sem,
 ):
     section = lax.axis_index("section")
     outer = lax.axis_index("outer")
@@ -382,7 +382,7 @@
     def share_sends(c):
         return [
             share_copy(c, mine_half, lane, target)
-            for lane, target in enumerate((far_inner, far_end, end))
+            for lane, target in enumerate((far_end, far_inner, end))
         ]
 
     def first(c):
@@ -446,6 +446,9 @@
             device_id_type=MESH,
         )
 
+    def result_copy(which):
+        return pltpu.make_async_copy(result.at[which], out_ref.at[which], result_sem.at[which])
+
     def send_final(which):
         for target in range(outers):
             final_out[which, target] = total[
@@ -505,10 +508,12 @@
         summed = final_in[which, 0].astype(F32)
         for origin in range(1, outers):
             summed = summed + final_in[which, origin].astype(F32)
-        out_ref[which] = summed.astype(BF16)
+        result[which] = summed.astype(BF16)
+        result_copy(which).start()
     for which in range(2):
         for target in range(outers):
             final_copy(which, outer, target).wait_send()
+        result_copy(which).wait()
 
 
 def part_out(both, out_ref, grad_ref):
@@ -528,7 +533,7 @@
         ),
         out_shape=jax.ShapeDtypeStruct((2, own_rows, model_width), BF16),
         in_specs=[pl.BlockSpec(memory_space=pl.ANY)] * 6,
-        out_specs=pl.BlockSpec(memory_space=pltpu.VMEM),
+        out_specs=pl.BlockSpec(memory_space=pl.ANY),
         scratch_shapes=[
             pltpu.VMEM((chunks, model_width, chunk), BF16),
             pltpu.VMEM((chunks, model_width, chunk), BF16),
@@ -546,6 +551,7 @@
             pltpu.VMEM((2, rows, model_width), F32),
             pltpu.VMEM((2, outers, own_rows, model_width), BF16),
             pltpu.VMEM((2, outers, own_rows, model_width), BF16),
+            pltpu.VMEM((2, own_rows, model_width), BF16),
             dma((3,)),
             dma((3, chunks)),
             dma((3, outers)),
@@ -557,6 +563,7 @@
             dma((chunks, 2)),
             dma((2, outers)),
             dma((2, outers)),
+            dma((2,)),
         ],
         compiler_params=pltpu.CompilerParams(
             collective_id=0, has_side_effects=True, vmem_limit_bytes=63 * 1024 * 1024

time: 40.3 us -> 40.1 us (level)
  no operation moved by 1% of the time
where the time goes in v3:
time: 40.1 us; the launch traced here: 39.9 us
  Pallas kernels  39.2 us (98%)
  between operations  0.64 us (2%)
    pallas_call x1, Pallas kernels, fast_call(): pl.pallas_call(functools.partial(fast_kernel, outers, tensors, chunks, ch...  37.8 us
    pallas_call x1, Pallas kernels, fast_call(): return pl.pallas_call(part_out, out_shape=(out, out))(both)  1.37 us

profile of v3, /device:TPU:0, one launch (start us, length us, event | category | flops | bytes accessed | tf_op | source)
XLA Modules:
  0.0 39.9 jit_solution(12758912672996606404)
XLA Ops:
  0.6 37.8 %shard_map.77.both = bf16[2,4,2048]{2,1,0:T(4,128)(2,1)} custom-call(bf16[1,4,2048]{2,1,0:T(4,128)(2,1)} %act.1, bf16[1,4,2048]{2,1,0:T(4,128)(2,1)} %saved.1, bf16[1,4,2048]{2,1,0:T(4,128)(2,1)} %cot.1, bf16[1,2048,3584]{2,1,0:T(8,128)(2,1)} %w_gate.1, bf16[1,2048,3584]{2,1,0:T(8,128)(2,1)} %w_up.1, bf16[1,3584,2048]{2,1,0:T(8,128)(2,1)} %w_down.1), custom_call_target="tpu_custom_call" | custom-call | tf_op jit(solution)/shard_map/pallas_call | solution.py:530
  38.5 1.4 %shard_map.78 = (bf16[1,4,2048]{2,1,0:T(4,128)(2,1)}, bf16[1,4,2048]{2,1,0:T(4,128)(2,1)}) custom-call(bf16[2,4,2048]{2,1,0:T(4,128)(2,1)} %shard_map.77.both), custom_call_target="tpu_custom_call" | custom-call | tf_op jit(solution)/shard_map/pallas_call | solution.py:573
